TPU v7x, 32 devices: a whole 2x2x4 slice. The times are simulated.
32 devices in a mesh: rows: 32 (over z, y, x, core).
Axes of the slice: x: 2, y: 2, z: 4, core: 2. Of those that a mesh axis runs over, the one named last changes fastest.
Arguments:
- snapshots: float32 [16384, 512], P('rows'), may hold values from -100 to 100
- validation: float32 [16384, 512], P('rows'), may hold values from -100 to 100
- eigenvectors: float32 [512, 64], replicated, may hold values from -0.25 to 0.25
- eigenvalues: float32 [64], replicated, may hold values from 16 to 256
Outputs:
- gram: float32 [512, 512], replicated
- modes: float32 [64, 16384], P(None, 'rows')
- train_coef: float32 [64, 512], replicated
- valid_coef: float32 [64, 512], replicated
All inputs are finite; a program needn't handle non-finite values.
Results may differ from a plain program's by a relative error of at most 0.000071.
Values sent between devices are 32-bit elements; how exact they have to be, the bound alone decides.
No kernel may reach another device: no remote copies, remote signals or barrier semaphores. Data moves between devices by JAX's collectives and lax.ppermute only.
A program may use at most 64 MiB of HBM per device.

v0:
```python
import jax
import jax.numpy as jnp
from jax import lax
from jax.sharding import PartitionSpec as P


def body(snapshots, validation, eigenvectors, eigenvalues):
    highest = lax.Precision.HIGHEST
    devices = lax.axis_size("rows")
    total = snapshots.shape[0] * devices * 1.0
    gram_part = (
        lax.dot_general(
            snapshots,
            snapshots,
            (((0,), (0,)), ((), ())),
            precision=highest,
            preferred_element_type=jnp.float32,
        )
        / total
    )
    scales = lax.rsqrt(eigenvalues)
    modes = (
        lax.dot_general(
            eigenvectors,
            snapshots,
            (((0,), (1,)), ((), ())),
            precision=highest,
            preferred_element_type=jnp.float32,
        )
        * scales[:, None]
    )
    gram = lax.psum(gram_part, "rows")
    valid_part = (
        jnp.dot(modes, validation, precision=highest, preferred_element_type=jnp.float32) / total
    )
    valid_coef = lax.psum(valid_part, "rows")
    train_coef = (
        lax.dot_general(
            eigenvectors,
            gram,
            (((0,), (0,)), ((), ())),
            precision=highest,
            preferred_element_type=jnp.float32,
        )
        * scales[:, None]
    )
    return (gram, modes, train_coef, valid_coef)


def solution(mesh):
    in_specs = (P("rows", None), P("rows", None), P(), P())
    out_specs = (P(), P(None, "rows"), P(), P())
    return jax.shard_map(body, mesh=mesh, in_specs=in_specs, out_specs=out_specs, check_vma=False)
```

profile of v0, /device:TPU:0, one launch (start us, length us, event | category | flops | bytes accessed | tf_op | source)
XLA Modules:
  0.0 159.9 jit_solution(1666710015621987377)
XLA Ops:
  7.2 0.0 copy-start
  7.2 0.0 all-reduce.3.cloned.1.call-start
  7.2 0.7 rsqrt.3
  8.0 0.4 copy-done
  8.4 0.0 copy-start.3
  8.4 2.8 %convolution_multiply_fusion = f32[512,512]{1,0:T(8,128)} fusion(f32[512,512]{1,0:T(8,128)S(1)} %copy-done), kind=kOutput, calls=%fused_computation | convolution fusion | flops 1610874880 | bytes 2097152 | tf_op jit(solution)/shard_map/dot_general | solution.py:12
  11.2 0.0 copy-done.3
  11.2 0.0 copy-start.2
  11.2 1.1 convolution_multiply_fusion.3
  12.4 0.1 copy-done.2
  12.5 0.0 copy-start.4
  12.5 1.4 convolution_multiply_fusion.1
  13.9 0.0 copy-done.4
  13.9 0.0 all-reduce.3.cloned.1.call-update
  13.9 134.7 %all-reduce.3.cloned.1.call-done = (f32[512,512]{1,0:T(8,128)}, f32[64,512]{1,0:T(8,128)}) async-done(((f32[512,512]{1,0:T(8,128)}, f32[64,512]{1,0:T(8,128)}), (f32[512,512]{1,0:T(8,128)}, f32[64,512]{1,0:T(8,128)})) %all-reduce.3.cloned.1.call-update) | async-done | bytes 1179664 | tf_op jit(solution)/shard_map/psum | solution.py:32
  148.7 0.0 copy-start.1
  148.7 2.8 %fusion = f32[64,512]{1,0:T(8,128)} fusion(f32[512,512]{1,0:T(8,128)} %get-tuple-element.6, f32[512,64]{0,1:T(8,128)S(1)} %copy-done.3, f32[64]{0:T(128)S(1)} %rsqrt.3), kind=kOutput, calls=%fused_computation.3 | convolution fusion | flops 201359360 | bytes 1310976 | tf_op jit(solution)/shard_map/dot_general | solution.py:38
  151.4 0.0 copy-done.1
  151.4 0.0 copy-start.5
  151.4 1.0 copy.10
  152.4 0.1 copy-done.5
  152.4 0.7 copy.11
Async XLA Ops:
  7.2 1.2 copy-start
  7.2 141.5 %all-reduce.3.cloned.1.call-start = ((), (), s32[]{:S(2)}) async-start(), calls=%async_computation | async-start | bytes 2359296 | tf_op jit(solution)/shard_map/psum | solution.py:32
  8.4 2.8 %copy-start.3 = (f32[512,64]{0,1:T(8,128)S(1)}, f32[512,64]{0,1:T(8,128)}, u32[]{:S(2)}) copy-start(f32[512,64]{0,1:T(8,128)} %param.6) | copy-start | bytes 393220
  11.2 1.2 copy-start.2
  12.5 1.4 copy-start.4
  148.7 2.8 %copy-start.1 = (f32[512,512]{1,0:T(8,128)S(1)}, f32[512,512]{1,0:T(8,128)}, u32[]{:S(2)}) copy-start(f32[512,512]{1,0:T(8,128)} %get-tuple-element.6) | copy-start | bytes 3145732
  151.4 1.0 copy-start.5
Sparse Core Ops, SparseCore 0:
  14.0 134.5 all-reduce.2
where the time goes:
time: 160 us
  waiting for transfers between devices  135 us (84%)
  between operations  14 us (9%)
  matrix products  8.12 us (5%)
  local copies, waits for them, and re-layouts  2.99 us (2%)
    psum x1, waiting for transfers between devices, body(): gram = lax.psum(gram_part, 'rows')  135 us
  transfers between devices with their start and end apart: 1, of which 1 were waited for; matrix products, arithmetic and copies ran while one was open for 0% of the time, Pallas kernels for 0%

commit v1 on v0

--- a/solution.py
+++ b/solution.py
@@ -29,7 +29,11 @@
         )
         * scales[:, None]
     )
-    gram = lax.psum(gram_part, "rows")
+    gram = gram_part
+    dev_count = lax.axis_size("rows")
+    for hop_no in [h for h in (1, 2, 4, 8, 16) if h < dev_count]:
+        back = lax.ppermute(gram, "rows", [(i0, i0 ^ hop_no) for i0 in range(dev_count)])
+        gram = gram + back
     valid_part = (
         jnp.dot(modes, validation, precision=highest, preferred_element_type=jnp.float32) / total
     )

time: 160 us -> 243 us (1.52)
  waiting for transfers between devices: 135 us -> 209 us
  starting transfers between devices: 0.04 us -> 9.3 us
    ppermute x0 -> x5, waiting for transfers between devices: none -> 113 us  [body(): lax.ppermute(gram, 'rows', [(i0, i0 ^ hop_no) for i0 in range(dev_count)])]
    psum x1, waiting for transfers between devices: 135 us -> 95.8 us  [body(): valid_coef = lax.psum(valid_part, 'rows')]
    ppermute x0 -> x5, starting transfers between devices: none -> 9.26 us  [body(): lax.ppermute(gram, 'rows', [(i0, i0 ^ hop_no) for i0 in range(dev_count)])]
  transfers between devices with their start and end apart: 1 -> 6, of which waited for: 1 -> 6; matrix products, arithmetic and copies ran while one was open for 0% -> 2% of each run, Pallas kernels for 0% -> 0%
where the time goes in v1:
time: 243 us
  waiting for transfers between devices  209 us (86%)
  between operations  14.1 us (6%)
  starting transfers between devices  9.3 us (4%)
  matrix products  5.85 us (2%)
  local copies, waits for them, and re-layouts  2.78 us (1%)
    ppermute x5, waiting for transfers between devices, body(): lax.ppermute(gram, 'rows', [(i0, i0 ^ hop_no) for i0 in range(dev_count)])  113 us
    psum x1, waiting for transfers between devices, body(): valid_coef = lax.psum(valid_part, 'rows')  95.8 us
    ppermute x5, starting transfers between devices, body(): lax.ppermute(gram, 'rows', [(i0, i0 ^ hop_no) for i0 in range(dev_count)])  9.26 us
  transfers between devices with their start and end apart: 6, of which 6 were waited for; matrix products, arithmetic and copies ran while one was open for 2% of the time, Pallas kernels for 0%

profile of v1, /device:TPU:0, one launch (start us, length us, event | category | flops | bytes accessed | tf_op | source)
XLA Modules:
  0.0 243.1 jit_solution(3521056402145835043)
XLA Ops:
  7.2 0.0 copy-start
  7.2 0.0 all-reduce.2.cloned.1.call-start
  7.2 1.2 copy-done
  8.4 1.9 convolution_multiply_fusion
  10.3 0.6 collective-permute-start
  10.8 2.3 collective-permute-done
  13.1 0.2 add.17
  13.3 2.9 %collective-permute-start.1 = (f32[512,512]{1,0:T(8,128)S(1)}, f32[512,512]{1,0:T(8,128)S(1)}, u32[]{:S(2)}, u32[]{:S(2)}) collective-permute-start(f32[512,512]{1,0:T(8,128)S(1)} %add.17), channel_id=1, source_target_pairs={{0,2},{1,3},{2,0},{3,1},{4,6},{5,7},{6,4},{7,5},{8,10},{9,11},{10,... | collective-permute-start | bytes 3145736 | tf_op jit(solution)/shard_map/ppermute | solution.py:35
  16.2 23.5 %collective-permute-done.1 = f32[512,512]{1,0:T(8,128)S(1)} collective-permute-done((f32[512,512]{1,0:T(8,128)S(1)}, f32[512,512]{1,0:T(8,128)S(1)}, u32[]{:S(2)}, u32[]{:S(2)}) %collective-permute-start.1) | collective-permute-done | bytes 1048608 | tf_op jit(solution)/shard_map/ppermute | solution.py:35
  39.7 0.2 add.18
  39.9 1.8 collective-permute-start.2
  41.7 22.9 %collective-permute-done.2 = f32[512,512]{1,0:T(8,128)S(1)} collective-permute-done((f32[512,512]{1,0:T(8,128)S(1)}, f32[512,512]{1,0:T(8,128)S(1)}, u32[]{:S(2)}, u32[]{:S(2)}) %collective-permute-start.2) | collective-permute-done | bytes 1048608 | tf_op jit(solution)/shard_map/ppermute | solution.py:35
  64.6 0.2 add.19
  64.8 0.0 copy-start.5
  64.8 0.0 copy-start.3
  64.8 1.6 collective-permute-start.3
  66.4 22.2 %collective-permute-done.3 = f32[512,512]{1,0:T(8,128)S(1)} collective-permute-done((f32[512,512]{1,0:T(8,128)S(1)}, f32[512,512]{1,0:T(8,128)S(1)}, u32[]{:S(2)}, u32[]{:S(2)}) %collective-permute-start.3) | collective-permute-done | bytes 1048608 | tf_op jit(solution)/shard_map/ppermute | solution.py:35
  88.7 0.2 add.20
  88.9 0.0 copy-start.2
  88.9 2.3 collective-permute-start.4
  91.2 0.0 copy-done.5
  91.2 0.0 copy-done.3
  91.2 1.1 convolution_multiply_fusion.3
  92.4 0.0 copy-done.2
  92.4 0.0 copy-start.4
  92.4 1.4 convolution_multiply_fusion.1
  93.8 0.0 copy-done.4
  93.8 0.0 all-reduce.2.cloned.1.call-update
  93.8 42.1 %collective-permute-done.4 = f32[512,512]{1,0:T(8,128)} collective-permute-done((f32[512,512]{1,0:T(8,128)S(1)}, f32[512,512]{1,0:T(8,128)}, u32[]{:S(2)}, u32[]{:S(2)}) %collective-permute-start.4) | collective-permute-done | bytes 1048608 | tf_op jit(solution)/shard_map/ppermute | solution.py:35
  136.0 1.4 add.21
  137.4 0.0 copy-start.1
  137.4 1.4 fusion
  138.8 95.8 %all-reduce.2.cloned.1.call-done = f32[64,512]{1,0:T(8,128)} async-done(((f32[64,512]{1,0:T(8,128)}), f32[64,512]{1,0:T(8,128)}) %all-reduce.2.cloned.1.call-update) | async-done | bytes 131088 | tf_op jit(solution)/shard_map/psum | solution.py:40
  234.7 1.6 copy.9
  236.2 0.0 copy-done.1
  (1 shorter events, 0.0 us)
Async XLA Ops:
  7.2 1.2 copy-start
  7.2 227.5 %all-reduce.2.cloned.1.call-start = ((), (), s32[]{:S(2)}) async-start(), calls=%async_computation | async-start | bytes 262144 | tf_op jit(solution)/shard_map/psum | solution.py:40
  10.3 2.8 %collective-permute-start = (f32[512,512]{1,0:T(8,128)S(1)}, f32[512,512]{1,0:T(8,128)S(1)}, u32[]{:S(2)}, u32[]{:S(2)}) collective-permute-start(f32[512,512]{1,0:T(8,128)S(1)} %convolution_multiply_fusion), channel_id=1, source_target_pairs={{0,1},{1,0},{2,3},{3,2},{4,5},{5,4},{6,7},{7,6},{8,9},{9,8},{10,11... | collective-permute-start | bytes 3145736 | tf_op jit(solution)/shard_map/ppermute | solution.py:35
  13.3 26.4 %collective-permute-start.1 = (f32[512,512]{1,0:T(8,128)S(1)}, f32[512,512]{1,0:T(8,128)S(1)}, u32[]{:S(2)}, u32[]{:S(2)}) collective-permute-start(f32[512,512]{1,0:T(8,128)S(1)} %add.17), channel_id=1, source_target_pairs={{0,2},{1,3},{2,0},{3,1},{4,6},{5,7},{6,4},{7,5},{8,10},{9,11},{10,... | collective-permute-start | bytes 3145736 | tf_op jit(solution)/shard_map/ppermute | solution.py:35
  39.9 24.7 %collective-permute-start.2 = (f32[512,512]{1,0:T(8,128)S(1)}, f32[512,512]{1,0:T(8,128)S(1)}, u32[]{:S(2)}, u32[]{:S(2)}) collective-permute-start(f32[512,512]{1,0:T(8,128)S(1)} %add.18), channel_id=1, source_target_pairs={{0,4},{1,5},{2,6},{3,7},{4,0},{5,1},{6,2},{7,3},{8,12},{9,13},{10,... | collective-permute-start | bytes 3145736 | tf_op jit(solution)/shard_map/ppermute | solution.py:35
  64.8 26.4 %copy-start.5 = (f32[64]{0:T(128)S(1)}, f32[64]{0:T(128)}, u32[]{:S(2)}) copy-start(f32[64]{0:T(128)} %param.7) | copy-start | bytes 772
  64.8 26.4 %copy-start.3 = (f32[512,64]{0,1:T(8,128)S(1)}, f32[512,64]{0,1:T(8,128)}, u32[]{:S(2)}) copy-start(f32[512,64]{0,1:T(8,128)} %param.6) | copy-start | bytes 393220
  64.8 23.8 %collective-permute-start.3 = (f32[512,512]{1,0:T(8,128)S(1)}, f32[512,512]{1,0:T(8,128)S(1)}, u32[]{:S(2)}, u32[]{:S(2)}) collective-permute-start(f32[512,512]{1,0:T(8,128)S(1)} %add.19), channel_id=1, source_target_pairs={{0,8},{1,9},{2,10},{3,11},{4,12},{5,13},{6,14},{7,15},{8,0},{9,1},... | collective-permute-start | bytes 3145736 | tf_op jit(solution)/shard_map/ppermute | solution.py:35
  88.9 3.5 %copy-start.2 = (f32[512,512]{1,0:T(8,128)S(1)}, f32[512,512]{1,0:T(8,128)}, u32[]{:S(2)}) copy-start(f32[512,512]{1,0:T(8,128)} %param.5) | copy-start | bytes 3145732
  88.9 47.1 %collective-permute-start.4 = (f32[512,512]{1,0:T(8,128)S(1)}, f32[512,512]{1,0:T(8,128)}, u32[]{:S(2)}, u32[]{:S(2)}) collective-permute-start(f32[512,512]{1,0:T(8,128)S(1)} %add.20), channel_id=1, source_target_pairs={{0,16},{1,17},{2,18},{3,19},{4,20},{5,21},{6,22},{7,23},{8,24},{9,... | collective-permute-start | bytes 3145736 | tf_op jit(solution)/shard_map/ppermute | solution.py:35
  92.4 1.4 copy-start.4
  137.4 98.8 %copy-start.1 = (f32[512,512]{1,0:T(8,128)}, f32[512,512]{1,0:T(8,128)S(1)}, u32[]{:S(2)}) copy-start(f32[512,512]{1,0:T(8,128)S(1)} %add.21) | copy-start | bytes 3145732
Sparse Core Ops, SparseCore 0:
  93.9 140.6 all-reduce.1
